TPU v7x, 256 devices: a whole 4x4x8 slice. The times are simulated.
256 devices in a mesh: seq: 64 (over y, z_lo, x), tp: 4 (over z_hi, core).
Axes of the slice: x: 4, y: 4, z: 8 (z_hi: 2, z_lo: 4; z = z_hi * 4 + z_lo), core: 2. Of those that a mesh axis runs over, the one named last changes fastest.
Arguments:
- hidden_in: bfloat16 [16384, 4096], P('seq', 'tp'), may hold values from -6 to 6
- order: int32 [16384], P('seq'), may hold values from 0 to 16383, as said below
- segment: int32 [16384], replicated, may hold values from 0 to 31, never falling along the last dimension, each value on 1 to 2048 neighbouring positions
- norm_gain: float32 [4096], replicated, may hold values from 0.1 to 1.9
- w_query: bfloat16 [4096, 2048], P('seq', 'tp')
- w_key: bfloat16 [4096, 512], P('seq', 'tp'), may hold values from -0.09375 to 0.09375
- w_value: bfloat16 [4096, 512], P('seq', 'tp'), may hold values from -0.09375 to 0.09375
- w_out: bfloat16 [2048, 4096], P('seq', 'tp'), may hold values from -0.5 to 0.5
Outputs:
- attn_out: bfloat16 [16384, 4096], P('seq', 'tp')
Inputs may be any that keep to these rules, and one draw needn't show every extreme that they name: order holds every position once; it is made of runs of 64 consecutive positions, each starting at a multiple of 64 and stored in rows that start at a multiple of 64. `segment`: never falls along positions.
All inputs are finite; a program needn't handle non-finite values.
Results may differ from a plain program's by a relative error of at most 0.014.
The roundings to bfloat16 on the way count: a program that leaves them out, or rounds other values in their place, can miss the bound.
Values may be sent and summed in bfloat16 or wider, within the bound.
No kernel may reach another device: no remote copies, remote signals or barrier semaphores. Data moves between devices by JAX's collectives and lax.ppermute only.
A program may use at most 128 MiB of HBM per device.

v0:
```python
import jax
import jax.numpy as jnp
from jax import lax
from jax.sharding import Mesh
from jax.sharding import PartitionSpec as P

HD = 128
SEQ = ("seq_0", "seq_1", "seq_2")
THETA = 500000.0
EPS = 1e-05


def sent_to_all(array, axis):
    copies = jnp.broadcast_to(array, (lax.axis_size(axis), *array.shape))
    return lax.all_to_all(copies, axis, split_axis=0, concat_axis=0, tiled=True)


def joined_along(blocks, dim):
    blocks = jnp.moveaxis(blocks, 0, dim)
    dims = blocks.shape
    return blocks.reshape(*dims[:dim], dims[dim] * dims[dim + 1], *dims[dim + 2 :])


def gather_directly(array, axis, dim):
    blocks = sent_to_all(array, axis)
    return joined_along(blocks, dim)


def side_by_side(arrays, axis, dim, along):
    widths = [a.shape[along] for a in arrays]
    both = jnp.concatenate(arrays, axis=along)
    filled = lax.all_gather(both, axis, axis=dim, tiled=True)
    return tuple(jnp.split(filled, [sum(widths[:k]) for k in range(1, len(widths))], axis=along))


def stacked_from(array, axes, sequence):
    blocks = array
    for k in sequence:
        blocks = lax.all_gather(blocks, axes[k])
    done = sequence[::-1]
    back = [done.index(k) for k in range(len(axes))]
    blocks = blocks.transpose(*back, *range(len(axes), blocks.ndim))
    return blocks.reshape(-1, *array.shape)


def gathered_by_axis(array, axes, sequence, dim):
    return joined_along(stacked_from(array, axes, sequence), dim)


def rotary(block, positions):
    head_dim = block.shape[-1]
    width = head_dim // 2
    frequency = THETA ** (-jnp.arange(width, dtype=jnp.float32) * 2.0 / head_dim)
    angle = positions.astype(jnp.float32)[:, None] * frequency[None, :]
    cosine = jnp.cos(angle)[:, None, :]
    sine = jnp.sin(angle)[:, None, :]
    first = block[..., :width]
    second = block[..., width:]
    return jnp.concatenate(
        [first * cosine - second * sine, second * cosine + first * sine], axis=-1
    )


def on_device(hidden_in, order, segment, norm_gain, w_query, w_key, w_value, w_out):
    rows = hidden_in.shape[0]
    whole = gather_directly(hidden_in, "tp", 1)
    wide = whole.astype(jnp.float32)
    mean_square = jnp.mean(wide * wide, axis=1, keepdims=True)
    normed = (wide * lax.rsqrt(mean_square + EPS) * norm_gain[None, :]).astype(jnp.bfloat16)
    pieces = side_by_side((w_query, w_key, w_value), SEQ, 0, 1)
    columns = normed
    query, key, value = tuple(
        (jnp.dot(columns, piece, preferred_element_type=jnp.float32) for piece in pieces)
    )
    heads_local = w_query.shape[1] // HD
    groups_local = w_key.shape[1] // HD
    group = heads_local // groups_local
    query = (rotary(query.reshape(rows, heads_local, HD), order) * HD ** (-0.5)).astype(
        jnp.bfloat16
    )
    query = query.reshape(rows, groups_local, group, HD)
    key = rotary(key.reshape(rows, groups_local, HD), order).astype(jnp.bfloat16)
    value = value.reshape(rows, groups_local, HD).astype(jnp.bfloat16)
    document = jnp.take(segment, order, axis=0)

    def attend(carry, block):
        key_block, value_block, key_order, key_document = block
        allowed = (key_order[None, :] <= order[:, None]) & (
            key_document[None, :] == document[:, None]
        )
        maximum, total, weighted = carry
        scores = jnp.einsum("rkgd,ckd->rkgc", query, key_block, preferred_element_type=jnp.float32)
        scores = jnp.where(allowed[:, None, None, :], scores, -jnp.inf)
        new_max = jnp.maximum(maximum, jnp.max(scores, axis=-1))
        anchor = jnp.where(new_max == -jnp.inf, 0.0, new_max)
        weights = jnp.exp(scores - anchor[..., None])
        shrink = jnp.exp(maximum - anchor)
        total = total * shrink + jnp.sum(weights, axis=-1)
        weighted = weighted * shrink[..., None] + jnp.einsum(
            "rkgc,ckd->rkgd",
            weights.astype(jnp.bfloat16),
            value_block,
            preferred_element_type=jnp.float32,
        )
        return (new_max, total, weighted)

    initial = (
        jnp.full((rows, groups_local, group), -jnp.inf, jnp.float32),
        jnp.zeros((rows, groups_local, group), jnp.float32),
        jnp.zeros((rows, groups_local, group, HD), jnp.float32),
    )
    carry = initial
    piece = (
        *side_by_side((key, value), SEQ, 0, 1),
        lax.all_gather(order, SEQ, axis=0, tiled=True),
        lax.all_gather(document, SEQ, axis=0, tiled=True),
    )
    count = piece[0].shape[0]
    stacked = tuple((member.reshape((count // 512, 512) + member.shape[1:]) for member in piece))
    carry, unused = lax.scan(lambda state, block: (attend(state, block), None), carry, stacked)
    maximum, total, weighted = carry
    mixed = (weighted / total[..., None]).reshape(rows, heads_local * HD).astype(jnp.bfloat16)
    every_head = gather_directly(mixed, "tp", 1)
    piece = gathered_by_axis(w_out, SEQ, (1, 0, 2), 0)
    columns = every_head
    result = jnp.dot(columns, piece, preferred_element_type=jnp.float32)
    return result.astype(jnp.bfloat16)


def solution(mesh):
    torus = Mesh(mesh.devices.reshape(4, 4, 4, mesh.shape["tp"]), ("seq_0", "seq_1", "seq_2", "tp"))
    placed = (
        P(SEQ, "tp"),
        P(SEQ),
        P(),
        P(),
        P(SEQ, "tp"),
        P(SEQ, "tp"),
        P(SEQ, "tp"),
        P(SEQ, "tp"),
    )
    return jax.shard_map(
        on_device, mesh=torus, in_specs=placed, out_specs=P(SEQ, "tp"), check_vma=False
    )
```

profile of v0, /device:TPU:1, one launch (start us, length us, event | category | flops | bytes accessed | tf_op | source)
XLA Modules:
  0.0 937.8 jit_solution(4467411417672132659)
XLA Ops:
  8.1 2.6 broadcast_in_dim.58
  10.8 9.9 %all-to-all-start = ((bf16[4,256,1024]{2,1,0:T(8,128)(2,1)}), bf16[4,256,1024]{2,1,0:T(8,128)(2,1)}, u32[]{:S(2)}, u32[]{:S(2)}) async-start(bf16[4,256,1024]{2,1,0:T(8,128)(2,1)} %broadcast_in_dim.58), calls=%async_computation | async-start | bytes 4194304 | tf_op jit(solution)/shard_map/all_to_all | solution.py:15
  20.7 67.4 %all-gather = bf16[128,1024]{1,0:T(8,128)(2,1)} all-gather(bf16[32,1024]{1,0:T(8,128)(2,1)S(1)} %copy-done.5), channel_id=2, replica_groups=mesh['seq_0'=4,'seq_1'=4,'seq_2'=4,'tp'=4] {'seq_1'}, dimensions={0}, use_global_device_ids=true | all-gather | bytes 327680 | tf_op jit(solution)/shard_map/all_gather | solution.py:39
  88.3 1.7 gather_fusion
  90.0 2.9 copy.37
  93.5 1.7 fusion.21
  95.2 248.8 %all-gather.10.cloned.1.call-done = bf16[4096,768]{1,0:T(8,128)(2,1)} async-done(((bf16[64,768]{1,0:T(8,128)(2,1)}), bf16[4096,768]{1,0:T(8,128)(2,1)}) %all-gather.10.cloned.1.call-update) | async-done | bytes 6291472 | tf_op jit(solution)/shard_map/all_gather | solution.py:32
  344.0 2.4 convolution_bitcast_fusion.1
  346.7 2.4 fusion.22
  349.9 159.7 %all-gather.4 = s32[64,1,256]{2,1,0:T(1,128)S(1)} all-gather(s32[1,1,256]{2,1,0:T(1,128)S(1)} %bitcast.141), channel_id=1, replica_groups=mesh['seq_0'=4,'seq_1'=4,'seq_2'=4,'tp'=4] {'seq_0','seq_1','seq_2'}, dimensions={0}, use_global_device_ids=true | all-gather | bytes 66560 | tf_op jit(solution)/shard_map/all_gather | solution.py:116
  509.8 155.2 %all-gather.3 = s32[64,1,256]{2,1,0:T(1,128)S(1)} all-gather(s32[1,1,256]{2,1,0:T(1,128)S(1)} %bitcast.140), channel_id=1, replica_groups=mesh['seq_0'=4,'seq_1'=4,'seq_2'=4,'tp'=4] {'seq_0','seq_1','seq_2'}, dimensions={0}, use_global_device_ids=true | all-gather | bytes 66560 | tf_op jit(solution)/shard_map/all_gather | solution.py:115
  665.6 1.7 multiply_convert_fusion
  667.3 4.5 slice_bitcast_fusion
  671.8 6.6 copy.39
  678.4 3.4 fusion.36
  682.2 5.1 fusion.34
  687.3 2.5 copy.52
  689.8 6.4 copy.48
  696.2 117.0 %while.15 = (s32[]{:T(128)}, f32[256,1,4]{0,2,1:T(4,128)S(1)}, f32[256,1,4]{0,2,1:T(4,128)S(1)}, f32[256,1,4,128]{0,3,2,1:T(8,128)S(1)}, s32[32,512]{1,0:T(8,128...) while((s32[]{:T(128)}, f32[256,1,4]{0,2,1:T(4,128)S(1)}, ...), condition=%wide.region_4.5_spmd.clone, body=%wide.region_1.4_spmd.clone.sunk | while | flops 273428480 | bytes 8476829 | solution.py:120
  698.2 1.6 fusion.56
  705.6 1.6 fusion.56
  709.2 1.6 fusion.56
  712.9 1.6 fusion.56
  720.2 1.6 fusion.56
  723.8 1.6 fusion.56
  727.5 1.6 fusion.56
  734.8 1.6 fusion.56
  738.5 1.6 fusion.56
  742.1 1.6 fusion.56
  749.4 1.6 fusion.56
  753.1 1.6 fusion.56
  756.8 1.6 fusion.56
  764.1 1.6 fusion.56
  767.8 1.6 fusion.56
  771.4 1.6 fusion.56
  775.1 1.6 fusion.56
  778.7 1.6 fusion.56
  782.4 1.6 fusion.56
  786.1 1.6 fusion.56
  789.7 1.6 fusion.56
  797.0 1.6 fusion.56
  800.7 1.6 fusion.56
  804.4 1.6 fusion.56
  811.7 1.6 fusion.56
  814.4 95.3 %all-to-all-start.1 = ((bf16[4,256,512]{1,2,0:T(8,128)(2,1)}), bf16[4,256,512]{1,2,0:T(8,128)(2,1)S(1)}, u32[]{:S(2)}, u32[]{:S(2)}) async-start(bf16[4,256,512]{1,2,0:T(8,128)(2,1)} %broadcast_in_dim.59), calls=%async_computation.1 | async-start | bytes 2097152 | tf_op jit(solution)/shard_map/all_to_all | solution.py:15
  909.7 5.0 copy.44
  914.7 12.4 %all-to-all-done.1 = bf16[4,256,512]{1,2,0:T(8,128)(2,1)S(1)} async-done(((bf16[4,256,512]{1,2,0:T(8,128)(2,1)}), bf16[4,256,512]{1,2,0:T(8,128)(2,1)S(1)}, u32[]{:S(2)}, u32[]{:S(2)}) %all-to-all-start.1) | async-done | bytes 1048608 | tf_op jit(solution)/shard_map/all_to_all | solution.py:15
  927.0 4.3 convolution_convert_fusion
  (310 shorter events, 80.8 us)
Async XLA Ops:
  6.5 81.7 %copy-start = (s32[16384]{0:T(1024)S(1)}, s32[16384]{0:T(1024)}, u32[]{:S(2)}) copy-start(s32[16384]{0:T(1024)} %param.12) | copy-start | bytes 196612
  6.5 14.2 %copy-start.5 = (bf16[32,1024]{1,0:T(8,128)(2,1)S(1)}, bf16[32,1024]{1,0:T(8,128)(2,1)}, u32[]{:S(2)}) copy-start(bf16[32,1024]{1,0:T(8,128)(2,1)} %param.17) | copy-start | bytes 196612
  6.5 81.7 %copy-start.3 = (s32[256]{0:T(256)S(1)}, s32[256]{0:T(256)}, u32[]{:S(2)}) copy-start(s32[256]{0:T(256)} %param.11) | copy-start | bytes 3076
  6.5 337.4 %all-gather.10.cloned.1.call-start = ((), (), s32[]{:S(2)}) async-start(), calls=%async_computation.2 | async-start | bytes 6389760 | tf_op jit(solution)/shard_map/all_gather | solution.py:32
  10.8 79.2 %all-to-all-start = ((bf16[4,256,1024]{2,1,0:T(8,128)(2,1)}), bf16[4,256,1024]{2,1,0:T(8,128)(2,1)}, u32[]{:S(2)}, u32[]{:S(2)}) async-start(bf16[4,256,1024]{2,1,0:T(8,128)(2,1)} %broadcast_in_dim.58), calls=%async_computation | async-start | bytes 4194304 | tf_op jit(solution)/shard_map/all_to_all | solution.py:15
  20.7 72.8 %copy-start.4 = (f32[4096]{0:T(1024)S(1)}, f32[4096]{0:T(1024)}, u32[]{:S(2)}) copy-start(f32[4096]{0:T(1024)} %param.13) | copy-start | bytes 49156
  20.7 644.9 %all-gather.14.cloned.1.call-start = ((), (), s32[]{:S(2)}) async-start(), calls=%async_computation.4 | async-start | bytes 1310720 | tf_op jit(solution)/shard_map/all_gather | solution.py:39
  88.2 594.0 %all-gather.12.cloned.1.call-start = ((), (), s32[]{:S(2)}) async-start(), calls=%async_computation.3 | async-start | bytes 8519680 | tf_op jit(solution)/shard_map/all_gather | solution.py:32
  349.8 559.8 %all-gather.16.cloned.1.call-start = ((), (), s32[]{:S(2)}) async-start(), calls=%async_computation.5 | async-start | bytes 5242880 | tf_op jit(solution)/shard_map/all_gather | solution.py:39
  671.8 6.6 copy-start.2
  814.4 112.7 %all-to-all-start.1 = ((bf16[4,256,512]{1,2,0:T(8,128)(2,1)}), bf16[4,256,512]{1,2,0:T(8,128)(2,1)S(1)}, u32[]{:S(2)}, u32[]{:S(2)}) async-start(bf16[4,256,512]{1,2,0:T(8,128)(2,1)} %broadcast_in_dim.59), calls=%async_computation.1 | async-start | bytes 2097152 | tf_op jit(solution)/shard_map/all_to_all | solution.py:15
  909.7 21.6 %copy-start.1 = (s32[16384]{0:T(1024)S(1)}, s32[16384]{0:T(1024)}, u32[]{:S(2)}) copy-start(s32[16384]{0:T(1024)} %param.12) | copy-start | bytes 196612
Sparse Core Ops, SparseCore 0:
  9.1 334.8 all-gather.9
  345.8 63.5 all-gather.13
  411.1 267.4 all-gather.11
  680.2 121.1 all-gather.15
where the time goes:
time: 940 us; the launch traced here: 938 us
  blocking collectives  382 us (41%)
  waiting for transfers between devices  261 us (28%)
  matrix products  106 us (11%)
  starting transfers between devices  105 us (11%)
  local copies, waits for them, and re-layouts  39.1 us (4%)
  other arithmetic  27.8 us (3%)
  between operations  13.3 us (1%)
    all_gather x2, waiting for transfers between devices, side_by_side(): filled = lax.all_gather(both, axis, axis=dim, tiled=True)  249 us
    all_gather x1, blocking collectives, on_device(): lax.all_gather(document, SEQ, axis=0, tiled=True)  160 us
    all_gather x1, blocking collectives, on_device(): lax.all_gather(order, SEQ, axis=0, tiled=True)  155 us
    all_to_all x2, starting transfers between devices, sent_to_all(): return lax.all_to_all(copies, axis, split_axis=0, concat_axis=0, tiled=True)  105 us
    all_gather x1, blocking collectives, stacked_from(): blocks = lax.all_gather(blocks, axes[k])  67.4 us
    dot_general x32, matrix products, attend(): jnp.einsum('rkgc,ckd->rkgd', weights.astype(jnp.bfloat16), value_block, p...  50.5 us
    dot_general x32, matrix products, attend(): jnp.einsum('rkgd,ckd->rkgc', query, key_block, preferred_element_type=jnp...  43.4 us
  transfers between devices with their start and end apart: 6, of which 2 were waited for; matrix products, arithmetic and copies ran while one was open for 18% of the time, Pallas kernels for 0%

commit v1 on v0

--- a/solution.py
+++ b/solution.py
@@ -8,6 +8,13 @@
 SEQ = ("seq_0", "seq_1", "seq_2")
 THETA = 500000.0
 EPS = 1e-05
+
+
+def swapped_in(value, axis, along):
+    size = lax.axis_size(axis)
+    blocks = jnp.stack([value for _ in range(size)])
+    blocks = lax.all_to_all(blocks, axis, split_axis=0, concat_axis=0)
+    return jnp.concatenate(blocks, axis=along)
 
 
 def sent_to_all(array, axis):
@@ -113,7 +120,7 @@
     piece = (
         *side_by_side((key, value), SEQ, 0, 1),
         lax.all_gather(order, SEQ, axis=0, tiled=True),
-        lax.all_gather(document, SEQ, axis=0, tiled=True),
+        swapped_in(document, SEQ, 0),
     )
     count = piece[0].shape[0]
     stacked = tuple((member.reshape((count // 512, 512) + member.shape[1:]) for member in piece))

time: 940 us -> 886 us (0.943)
  blocking collectives: 382 us -> 228 us
  waiting for transfers between devices: 261 us -> 411 us
  starting transfers between devices: 105 us -> 55.6 us
    all_gather x1 -> x0, blocking collectives: 160 us -> none  [on_device(): lax.all_gather(document, SEQ, axis=0, tiled=True)]
    all_gather x2, waiting for transfers between devices: 249 us -> 391 us  [side_by_side(): filled = lax.all_gather(both, axis, axis=dim, tiled=True)]
    all_to_all x2, starting transfers between devices: 105 us -> 47.3 us  [sent_to_all(): return lax.all_to_all(copies, axis, split_axis=0, concat_axis=0, tiled=True)]
  transfers between devices with their start and end apart: 6 -> 7, of which waited for: 2 -> 3; matrix products, arithmetic and copies ran while one was open for 18% -> 19% of each run, Pallas kernels for 0% -> 0%
where the time goes in v1:
time: 886 us; the launch traced here: 884 us
  waiting for transfers between devices  411 us (46%)
  blocking collectives  228 us (26%)
  matrix products  106 us (12%)
  starting transfers between devices  55.6 us (6%)
  local copies, waits for them, and re-layouts  39.7 us (4%)
  other arithmetic  27.8 us (3%)
  between operations  13.4 us (2%)
    all_gather x2, waiting for transfers between devices, side_by_side(): filled = lax.all_gather(both, axis, axis=dim, tiled=True)  391 us
    all_gather x1, blocking collectives, on_device(): lax.all_gather(order, SEQ, axis=0, tiled=True)  161 us
    all_gather x1, blocking collectives, stacked_from(): blocks = lax.all_gather(blocks, axes[k])  67.4 us
    dot_general x32, matrix products, attend(): jnp.einsum('rkgc,ckd->rkgd', weights.astype(jnp.bfloat16), value_block, p...  50.5 us
    all_to_all x2, starting transfers between devices, sent_to_all(): return lax.all_to_all(copies, axis, split_axis=0, concat_axis=0, tiled=True)  47.3 us
    dot_general x32, matrix products, attend(): jnp.einsum('rkgd,ckd->rkgc', query, key_block, preferred_element_type=jnp...  43.4 us
    all_to_all x2, waiting for transfers between devices, sent_to_all(): return lax.all_to_all(copies, axis, split_axis=0, concat_axis=0, tiled=True)  19.2 us
  transfers between devices with their start and end apart: 7, of which 3 were waited for; matrix products, arithmetic and copies ran while one was open for 19% of the time, Pallas kernels for 0%

profile of v1, /device:TPU:1, one launch (start us, length us, event | category | flops | bytes accessed | tf_op | source)
XLA Modules:
  0.0 883.7 jit_solution(508804764846708839)
XLA Ops:
  8.1 2.6 broadcast_in_dim.58
  10.8 9.9 %all-to-all-start.1 = ((bf16[4,256,1024]{2,1,0:T(8,128)(2,1)}), bf16[4,256,1024]{2,1,0:T(8,128)(2,1)}, u32[]{:S(2)}, u32[]{:S(2)}) async-start(bf16[4,256,1024]{2,1,0:T(8,128)(2,1)} %broadcast_in_dim.58), calls=%async_computation.1 | async-start | bytes 4194304 | tf_op jit(solution)/shard_map/all_to_all | solution.py:22
  20.7 67.4 %all-gather = bf16[128,1024]{1,0:T(8,128)(2,1)} all-gather(bf16[32,1024]{1,0:T(8,128)(2,1)S(1)} %copy-done.5), channel_id=2, replica_groups=mesh['seq_0'=4,'seq_1'=4,'seq_2'=4,'tp'=4] {'seq_1'}, dimensions={0}, use_global_device_ids=true | all-gather | bytes 327680 | tf_op jit(solution)/shard_map/all_gather | solution.py:46
  88.3 1.7 gather_fusion
  90.0 2.9 copy.37
  93.5 1.7 fusion.21
  95.2 248.7 %all-gather.9.cloned.1.call-done = bf16[4096,768]{1,0:T(8,128)(2,1)} async-done(((bf16[64,768]{1,0:T(8,128)(2,1)}), bf16[4096,768]{1,0:T(8,128)(2,1)}) %all-gather.9.cloned.1.call-update) | async-done | bytes 6291472 | tf_op jit(solution)/shard_map/all_gather | solution.py:39
  343.9 2.4 convolution_bitcast_fusion.1
  346.7 2.4 fusion.22
  350.5 8.3 all-to-all-start
  358.9 160.5 %all-gather.3 = s32[64,1,256]{2,1,0:T(1,128)S(1)} all-gather(s32[1,1,256]{2,1,0:T(1,128)S(1)} %bitcast.139), channel_id=1, replica_groups=mesh['seq_0'=4,'seq_1'=4,'seq_2'=4,'tp'=4] {'seq_0','seq_1','seq_2'}, dimensions={0}, use_global_device_ids=true | all-gather | bytes 66560 | tf_op jit(solution)/shard_map/all_gather | solution.py:122
  520.2 1.7 multiply_convert_fusion
  521.9 4.5 slice_bitcast_fusion
  526.4 6.5 copy.39
  532.9 3.5 fusion.36
  536.7 142.6 %all-gather.11.cloned.1.call-done = bf16[16384,2,128]{0,2,1:T(8,128)(2,1)} async-done(((bf16[256,2,128]{0,2,1:T(8,128)(2,1)}), bf16[16384,2,128]{0,2,1:T(8,128)(2,1)}) %all-gather.11.cloned.1.call-update) | async-done | bytes 8388624 | tf_op jit(solution)/shard_map/all_gather | solution.py:39
  679.3 5.1 fusion.34
  684.4 2.5 copy.52
  686.9 6.4 copy.48
  693.3 117.1 %while.15 = (s32[]{:T(128)}, f32[256,1,4]{0,2,1:T(4,128)S(1)}, f32[256,1,4]{0,2,1:T(4,128)S(1)}, f32[256,1,4,128]{0,3,2,1:T(8,128)S(1)}, s32[32,512]{1,0:T(8,128...) while((s32[]{:T(128)}, f32[256,1,4]{0,2,1:T(4,128)S(1)}, ...), condition=%wide.region_4.5_spmd.clone, body=%wide.region_1.4_spmd.clone.sunk | while | flops 273428480 | bytes 8476829 | solution.py:127
  695.3 1.6 fusion.56
  699.0 1.6 fusion.56
  702.6 1.6 fusion.56
  709.9 1.6 fusion.56
  713.6 1.6 fusion.56
  717.3 1.6 fusion.56
  724.6 1.6 fusion.56
  731.9 1.6 fusion.56
  735.6 1.6 fusion.56
  739.2 1.6 fusion.56
  742.9 1.6 fusion.56
  746.6 1.6 fusion.56
  750.2 1.6 fusion.56
  753.9 1.6 fusion.56
  761.2 1.6 fusion.56
  764.9 1.6 fusion.56
  768.5 1.6 fusion.56
  775.8 1.6 fusion.56
  779.5 1.6 fusion.56
  783.1 1.6 fusion.56
  790.5 1.6 fusion.56
  794.1 1.6 fusion.56
  797.8 1.6 fusion.56
  808.7 1.6 fusion.56
  811.5 37.3 %all-to-all-start.2 = ((bf16[4,256,512]{1,2,0:T(8,128)(2,1)}), bf16[4,256,512]{1,2,0:T(8,128)(2,1)S(1)}, u32[]{:S(2)}, u32[]{:S(2)}) async-start(bf16[4,256,512]{1,2,0:T(8,128)(2,1)} %broadcast_in_dim.59), calls=%async_computation.2 | async-start | bytes 2097152 | tf_op jit(solution)/shard_map/all_to_all | solution.py:22
  848.8 5.0 copy.44
  853.8 19.2 %all-to-all-done.2 = bf16[4,256,512]{1,2,0:T(8,128)(2,1)S(1)} async-done(((bf16[4,256,512]{1,2,0:T(8,128)(2,1)}), bf16[4,256,512]{1,2,0:T(8,128)(2,1)S(1)}, u32[]{:S(2)}, u32[]{:S(2)}) %all-to-all-start.2) | async-done | bytes 1048608 | tf_op jit(solution)/shard_map/all_to_all | solution.py:22
  872.9 4.3 convolution_convert_fusion
  (312 shorter events, 83.1 us)
Async XLA Ops:
  6.5 81.7 %copy-start = (s32[16384]{0:T(1024)S(1)}, s32[16384]{0:T(1024)}, u32[]{:S(2)}) copy-start(s32[16384]{0:T(1024)} %param.12) | copy-start | bytes 196612
  6.5 14.2 %copy-start.5 = (bf16[32,1024]{1,0:T(8,128)(2,1)S(1)}, bf16[32,1024]{1,0:T(8,128)(2,1)}, u32[]{:S(2)}) copy-start(bf16[32,1024]{1,0:T(8,128)(2,1)} %param.17) | copy-start | bytes 196612
  6.5 81.7 %copy-start.3 = (s32[256]{0:T(256)S(1)}, s32[256]{0:T(256)}, u32[]{:S(2)}) copy-start(s32[256]{0:T(256)} %param.11) | copy-start | bytes 3076
  6.5 337.4 %all-gather.9.cloned.1.call-start = ((), (), s32[]{:S(2)}) async-start(), calls=%async_computation.3 | async-start | bytes 6389760 | tf_op jit(solution)/shard_map/all_gather | solution.py:39
  10.8 79.3 %all-to-all-start.1 = ((bf16[4,256,1024]{2,1,0:T(8,128)(2,1)}), bf16[4,256,1024]{2,1,0:T(8,128)(2,1)}, u32[]{:S(2)}, u32[]{:S(2)}) async-start(bf16[4,256,1024]{2,1,0:T(8,128)(2,1)} %broadcast_in_dim.58), calls=%async_computation.1 | async-start | bytes 4194304 | tf_op jit(solution)/shard_map/all_to_all | solution.py:22
  20.7 72.8 %copy-start.4 = (f32[4096]{0:T(1024)S(1)}, f32[4096]{0:T(1024)}, u32[]{:S(2)}) copy-start(f32[4096]{0:T(1024)} %param.13) | copy-start | bytes 49156
  20.7 499.4 %all-gather.13.cloned.1.call-start = ((), (), s32[]{:S(2)}) async-start(), calls=%async_computation.5 | async-start | bytes 1310720 | tf_op jit(solution)/shard_map/all_gather | solution.py:46
  88.2 591.1 %all-gather.11.cloned.1.call-start = ((), (), s32[]{:S(2)}) async-start(), calls=%async_computation.4 | async-start | bytes 8519680 | tf_op jit(solution)/shard_map/all_gather | solution.py:39
  350.5 169.4 %all-to-all-start = ((s32[64,1,256]{2,1,0:T(1,128)}), s32[64,1,256]{2,1,0:T(1,128)S(1)}, u32[]{:S(2)}, u32[]{:S(2)}) async-start(s32[64,1,256]{2,1,0:T(1,128)} %stack.2), calls=%async_computation | async-start | bytes 131072 | tf_op jit(solution)/shard_map/all_to_all | solution.py:16
  358.8 490.0 %all-gather.15.cloned.1.call-start = ((), (), s32[]{:S(2)}) async-start(), calls=%async_computation.6 | async-start | bytes 5242880 | tf_op jit(solution)/shard_map/all_gather | solution.py:46
  526.4 6.5 copy-start.2
  811.5 61.5 %all-to-all-start.2 = ((bf16[4,256,512]{1,2,0:T(8,128)(2,1)}), bf16[4,256,512]{1,2,0:T(8,128)(2,1)S(1)}, u32[]{:S(2)}, u32[]{:S(2)}) async-start(bf16[4,256,512]{1,2,0:T(8,128)(2,1)} %broadcast_in_dim.59), calls=%async_computation.2 | async-start | bytes 2097152 | tf_op jit(solution)/shard_map/all_to_all | solution.py:22
  848.8 28.4 %copy-start.1 = (s32[16384]{0:T(1024)S(1)}, s32[16384]{0:T(1024)}, u32[]{:S(2)}) copy-start(s32[16384]{0:T(1024)} %param.12) | copy-start | bytes 196612
Sparse Core Ops, SparseCore 0:
  9.1 334.7 all-gather.8
  345.7 63.8 all-gather.12
  411.4 267.9 all-gather.10
  681.0 80.5 all-gather.14
